TPU v7x, 256 devices: a 4x2x16 block of a 4x16x16 slice. The times are simulated.
256 devices in a mesh: parts: 2 (over y), expert: 16 (over z), tensor: 4 (over x), seq: 2 (over core).
Axes of the slice: x: 4, y: 2, z: 16, core: 2. Of those that a mesh axis runs over, the one named last changes fastest.
The devices are a block of a 4x16x16 slice.
Arguments:
- tokens: bfloat16 [1024, 4096], P(('parts', 'expert', 'tensor', 'seq')), parts along dimension 0, may hold values from -6 to 6
- out_grad: bfloat16 [1024, 4096], P(('parts', 'expert', 'tensor', 'seq')), parts along dimension 0, may hold values from -3 to 3
- expert_ids: int32 [1024, 2], P(('parts', 'expert', 'tensor', 'seq')), parts along dimension 0, may hold values from 0 to 3, all different within a row; in each aligned block of 4 rows (0 to 3, 4 to 7, ...) at most 3 rows name the same one
- probs: bfloat16 [1024, 2], P(('parts', 'expert', 'tensor', 'seq')), parts along dimension 0, may hold values from 0.19921875 to 1
- w_gate: bfloat16 [16, 4096, 2048], P('expert', None, ('tensor', 'seq')), may hold values from -0.09375 to 0.09375
- w_up: bfloat16 [16, 4096, 2048], P('expert', None, ('tensor', 'seq')), may hold values from -0.09375 to 0.09375
- w_down: bfloat16 [16, 2048, 4096], P('expert', ('tensor', 'seq')), may hold values from -0.0625 to 0.0625
Outputs:
- grad_tokens: float32 [1024, 4096], P(('parts', 'expert', 'tensor', 'seq')), parts along dimension 0
- grad_probs: float32 [1024, 2], P(('parts', 'expert', 'tensor', 'seq')), parts along dimension 0
- grad_gate: bfloat16 [32, 4096, 2048], P(('parts', 'expert'), None, ('tensor', 'seq')), parts along dimension 0
- grad_up: bfloat16 [32, 4096, 2048], P(('parts', 'expert'), None, ('tensor', 'seq')), parts along dimension 0
- grad_down: bfloat16 [32, 2048, 4096], P(('parts', 'expert'), ('tensor', 'seq')), parts along dimension 0
There are 2 independent parts, one for each index of `parts`. A program takes and returns all parts, laid end to end along the dimension named above; an argument that names none is the same for every part. Nothing has to cross between parts.
Inputs may be any that keep to these rules, and one draw needn't show every extreme that they name: `expert_ids`: each row names 2 different experts. Within the rows of one device (aligned blocks of 4 rows) no expert is named by more than 3 rows, a bound that some block reaches.
All inputs are finite; a program needn't handle non-finite values.
Results may differ from a plain program's by a relative error of at most 0.005.
Values may be sent and summed in bfloat16 or wider, within the bound.
A program may use at most 128 MiB of HBM per device.

v0:
```python
import math

import jax
import jax.numpy as jnp
from jax import lax
from jax.sharding import PartitionSpec as P

EXPERTS = 4
TOP = 2
CAP = 3


def sent_together(arrays, axis, split_dim, concat_dim, along):
    columns = [a.reshape(*a.shape[:along], -1) for a in arrays]
    both = jnp.concatenate(columns, axis=along)
    result, at, gathered = (
        lax.all_to_all(both, axis, split_axis=split_dim, concat_axis=concat_dim, tiled=True),
        0,
        [],
    )
    for a, column in zip(arrays, columns):
        share = result[..., at : at + column.shape[along]]
        gathered.append(share.reshape(*share.shape[:along], *a.shape[along:]))
        at += column.shape[along]
    return tuple(gathered)


def in_one_piece(arrays, axis, dim, along):
    widths = [math.prod(a.shape[along:]) for a in arrays]
    both = jnp.concatenate(
        [a.reshape(*a.shape[:along], w) for a, w in zip(arrays, widths)], axis=along
    )
    result = lax.all_gather(both, axis, axis=dim, tiled=True)
    blocks = jnp.split(result, [sum(widths[:k]) for k in range(1, len(widths))], axis=along)
    return tuple(
        (b.reshape(*result.shape[:along], *a.shape[along:]) for a, b in zip(arrays, blocks))
    )


def silu_parts(gate):
    sigma = jax.nn.sigmoid(gate)
    return (gate * sigma, sigma * (1.0 + gate * (1.0 - sigma)))


def repeat_owners(block, copies):
    shape = block.shape
    wide = jnp.broadcast_to(block[:, None], (shape[0], copies) + shape[1:])
    return wide.reshape((shape[0] * copies,) + shape[1:])


def contract(left, right, left_dim, right_dim):
    return lax.dot_general(
        left, right, (((left_dim,), (right_dim,)), ((), ())), preferred_element_type=jnp.float32
    )


def per_device(tokens, out_grad, expert_ids, probs, w_gate, w_up, w_down):
    owners = lax.axis_size("expert")
    holders = lax.axis_size(("tensor", "seq"))
    split = owners // EXPERTS
    width = tokens.shape[1]
    count = tokens.shape[0]
    flat = expert_ids.reshape(-1)
    onehot = (flat[:, None] == jnp.arange(EXPERTS, dtype=jnp.int32)[None, :]).astype(jnp.int32)
    before = jnp.cumsum(onehot, axis=0) - onehot
    target = flat * CAP + jnp.sum(before * onehot, axis=1)
    places = jnp.arange(EXPERTS * CAP, dtype=jnp.int32)
    hits = places[:, None] == target[None, :]
    select = jnp.any(hits.reshape(EXPERTS * CAP, count, TOP), axis=2).astype(jnp.bfloat16)
    packed_x = (
        jnp.dot(select, tokens, preferred_element_type=jnp.float32)
        .astype(jnp.bfloat16)
        .reshape(EXPERTS, CAP, width)
    )
    packed_dy = (
        jnp.dot(select, out_grad, preferred_element_type=jnp.float32)
        .astype(jnp.bfloat16)
        .reshape(EXPERTS, CAP, width)
    )
    weights_flat = probs.reshape(-1).astype(jnp.float32)
    packed_p = (
        jnp.sum(jnp.where(hits, weights_flat[None, :], 0.0), axis=1)
        .astype(jnp.bfloat16)
        .reshape(EXPERTS, CAP)
    )
    owner_x, owner_dy, owner_p = sent_together(
        (
            repeat_owners(packed_x, split),
            repeat_owners(packed_dy, split),
            repeat_owners(packed_p, split),
        ),
        "expert",
        0,
        0,
        2,
    )
    rows_x, rows_dy, rows_p = in_one_piece(
        (owner_x[:, None], owner_dy[:, None], owner_p[:, None]), ("tensor", "seq"), 1, 3
    )
    inputs = rows_x.reshape(-1, width)
    cotangent = rows_dy.reshape(-1, width)
    scale = rows_p.reshape(-1, 1).astype(jnp.float32)
    w_g = w_gate[0]
    w_u = w_up[0]
    w_d = w_down[0]
    gate = jnp.dot(inputs, w_g, preferred_element_type=jnp.float32)
    up = jnp.dot(inputs, w_u, preferred_element_type=jnp.float32)
    back = contract(cotangent, w_d, 1, 1)
    act, slope = silu_parts(gate)
    hidden = act * up
    score = jnp.sum(back * hidden, axis=1)
    scaled = scale * back
    d_gate = (scaled * up * slope).astype(jnp.bfloat16)
    d_up = (scaled * act).astype(jnp.bfloat16)
    weighted = (scale * hidden).astype(jnp.bfloat16)
    part_dx = contract(d_gate, w_g, 1, 1) + contract(d_up, w_u, 1, 1)
    grad_g = contract(inputs, d_gate, 0, 0).astype(jnp.bfloat16)[None]
    grad_u = contract(inputs, d_up, 0, 0).astype(jnp.bfloat16)[None]
    grad_d = contract(weighted, cotangent, 0, 0).astype(jnp.bfloat16)[None]
    kept_dx, kept_score = (
        lax.psum_scatter(
            part_dx.reshape(owners, holders, CAP, width),
            ("tensor", "seq"),
            scatter_dimension=1,
            tiled=True,
        ),
        lax.psum_scatter(
            score.reshape(owners, holders, CAP), ("tensor", "seq"), scatter_dimension=1, tiled=True
        ),
    )
    got_dx, got_score = sent_together((kept_dx[:, 0], kept_score[:, 0]), "expert", 0, 0, 2)
    total_dx = jnp.sum(got_dx.reshape(EXPERTS, split, CAP, width), axis=1).reshape(
        EXPERTS * CAP, width
    )
    total_score = jnp.sum(got_score.reshape(EXPERTS, split, CAP), axis=1).reshape(-1)
    grad_tokens = jnp.sum(jnp.take(total_dx, target, axis=0).reshape(count, TOP, width), axis=1)
    grad_probs = jnp.take(total_score, target, axis=0).reshape(count, TOP)
    return (grad_tokens, grad_probs, grad_g, grad_u, grad_d)


def solution(mesh):
    placed = (
        P(("parts", "expert", "tensor", "seq"), None),
        P(("parts", "expert", "tensor", "seq"), None),
        P(("parts", "expert", "tensor", "seq"), None),
        P(("parts", "expert", "tensor", "seq"), None),
        P("expert", None, ("tensor", "seq")),
        P("expert", None, ("tensor", "seq")),
        P("expert", ("tensor", "seq"), None),
    )
    return jax.shard_map(
        per_device,
        mesh=mesh,
        in_specs=placed,
        out_specs=(
            P(("parts", "expert", "tensor", "seq"), None),
            P(("parts", "expert", "tensor", "seq"), None),
            P(("parts", "expert"), None, ("tensor", "seq")),
            P(("parts", "expert"), None, ("tensor", "seq")),
            P(("parts", "expert"), ("tensor", "seq"), None),
        ),
        check_vma=False,
    )
```

profile of v0, /device:TPU:33, one launch (start us, length us, event | category | flops | bytes accessed | tf_op | source)
XLA Modules:
  0.0 322.5 jit_solution(12563170055464449671)
XLA Ops:
  12.7 78.7 %all_to_all.10 = bf16[16,3,8193]{2,1,0:T(4,128)(2,1)S(1)} all-to-all(bf16[16,3,8193]{2,1,0:T(4,128)(2,1)S(1)} %copy.148), channel_id=1, replica_groups=mesh['parts'=2,'expert'=16,'tensor'=4,'seq'=2] {'expert'}, dimensions={0} | all-to-all | bytes 1573056 | tf_op jit(solution)/shard_map/all_to_all | solution.py:17
  93.8 42.1 %all-gather.2.cloned.1.call-done = bf16[16,8,3,8193]{3,0,2,1:T(8,128)(2,1)} async-done(((bf16[16,1,3,8193]{3,0,2,1:T(8,128)(2,1)}), bf16[16,8,3,8193]{3,0,2,1:T(8,128)(2,1)}) %all-gather.2.cloned.1.call-update) | async-done | bytes 6292240 | tf_op jit(solution)/shard_map/all_gather | solution.py:33
  136.0 5.2 %fusion.20 = (bf16[16,8,3,4096]{3,0,2,1:T(8,128)(2,1)S(1)}, bf16[16,8,3,4096]{3,0,2,1:T(8,128)(2,1)}) fusion(bf16[16,8,3,8193]{3,0,2,1:T(8,128)(2,1)} %all-gather.2.cloned.1.call-done), kind=kLoop, calls=%fused_computation.53 | loop fusion | bytes 12582912 | tf_op jit(solution)/shard_map/split | solution.py:34
  141.2 4.7 %copy.155 = bf16[16,8,3,4096]{3,2,1,0:T(4,128)(2,1)} copy(bf16[16,8,3,4096]{3,0,2,1:T(8,128)(2,1)S(1)} %get-tuple-element.47) | data formatting | bytes 6291456 | tf_op jit(solution)/shard_map/split | solution.py:34
  145.9 7.4 %reshape.133 = bf16[384,4096]{1,0:T(8,128)(2,1)} reshape(bf16[16,8,3,4096]{3,2,1,0:T(4,128)(2,1)} %copy.155) | data formatting | bytes 6291456 | tf_op jit(solution)/shard_map/reshape | solution.py:100
  153.4 6.6 %copy.154 = bf16[16,8,3,4096]{3,2,1,0:T(4,128)(2,1)} copy(bf16[16,8,3,4096]{3,0,2,1:T(8,128)(2,1)} %get-tuple-element.48) | data formatting | bytes 6291456 | tf_op jit(solution)/shard_map/split | solution.py:34
  160.0 7.5 %reshape.132 = bf16[384,4096]{1,0:T(8,128)(2,1)} reshape(bf16[16,8,3,4096]{3,2,1,0:T(4,128)(2,1)} %copy.154) | data formatting | bytes 6291456 | tf_op jit(solution)/shard_map/reshape | solution.py:101
  168.0 4.0 %fusion.8 = f32[384,256]{0,1:T(8,128)S(1)} fusion(bf16[384,4096]{1,0:T(8,128)(2,1)} %reshape.133, bf16[1,4096,256]{2,1,0:T(8,128)(2,1)} %param.12), kind=kOutput, calls=%fused_computation.16 | convolution fusion | flops 805306368 | bytes 5636096 | tf_op jit(solution)/shard_map/dot_general | solution.py:107
  172.1 1.3 fusion.10
  174.2 2.1 multiply_convert_fusion.2
  178.0 3.7 %convolution_add_fusion = f32[384,4096]{1,0:T(8,128)} fusion(f32[384,4096]{1,0:T(8,128)S(1)} %fusion.3, bf16[384,256]{0,1:T(8,128)(2,1)S(1)} %get-tuple-element.53, bf16[1,4096,256]{2,1,0:T(8,128)(2,1)S(1)} %copy-done.6), kind=kOutput, calls=%fused_computation.2 | convolution fusion | flops 806879232 | bytes 14876672 | tf_op jit(solution)/shard_map/dot_general | solution.py:52
  181.7 9.1 %reshape.134 = f32[16,8,3,4096]{3,2,1,0:T(4,128)} reshape(f32[384,4096]{1,0:T(8,128)} %convolution_add_fusion) | data formatting | bytes 12582912 | tf_op jit(solution)/shard_map/reshape | solution.py:122
  190.8 9.7 %copy.156 = f32[16,8,3,4096]{3,0,2,1:T(8,128)} copy(f32[16,8,3,4096]{3,2,1,0:T(4,128)} %reshape.134) | data formatting | bytes 12582912 | tf_op jit(solution)/shard_map/reshape | solution.py:122
  202.1 21.0 %all-reduce = f32[16,8,3]{0,2,1:T(4,128)S(1)} all-reduce(f32[16,8,3]{0,2,1:T(4,128)S(1)} %copy.157), channel_id=3, replica_groups=mesh['parts'=2,'expert'=16,'tensor'=4,'seq'=2] {'tensor','seq'}, use_global_device_ids=true, to_apply=%region_6.7.clone | all-reduce | flops 384 | bytes 3072
  223.8 24.7 %reduce-scatter.2.cloned.1.call-done = f32[16,1,3,4096]{3,0,2,1:T(8,128)} async-done(((f32[16,8,3,4096]{3,0,2,1:T(8,128)}), f32[16,1,3,4096]{3,0,2,1:T(8,128)}) %reduce-scatter.2.cloned.1.call-update) | async-done | bytes 786448 | tf_op jit(solution)/shard_map/reduce_scatter | solution.py:121
  248.5 1.2 pad_maximum_fusion.1
  249.7 1.4 copy.159
  251.1 12.1 %all-to-all-start.1 = ((f32[16,3,4097]{2,1,0:T(4,128)}), f32[16,3,4097]{2,1,0:T(4,128)S(1)}, u32[]{:S(2)}, u32[]{:S(2)}) async-start(f32[16,3,4097]{2,1,0:T(4,128)} %copy.159), calls=%async_computation.2 | async-start | bytes 2162688 | tf_op jit(solution)/shard_map/all_to_all | solution.py:17
  263.3 4.7 %fusion = bf16[1,4096,256]{2,1,0:T(8,128)(2,1)} fusion(bf16[384,4096]{1,0:T(8,128)(2,1)} %reshape.133, bf16[384,256]{0,1:T(8,128)(2,1)S(1)} %get-tuple-element.49), kind=kOutput, calls=%fused_computation.6 | convolution fusion | flops 806354944 | bytes 5439488 | tf_op jit(solution)/shard_map/dot_general | solution.py:52
  268.0 2.6 fusion.1
  270.6 2.6 fusion.2
  273.2 35.6 %all-to-all-done.1 = f32[16,3,4097]{2,1,0:T(4,128)S(1)} async-done(((f32[16,3,4097]{2,1,0:T(4,128)}), f32[16,3,4097]{2,1,0:T(4,128)S(1)}, u32[]{:S(2)}, u32[]{:S(2)}) %all-to-all-start.1) | async-done | bytes 786656 | tf_op jit(solution)/shard_map/all_to_all | solution.py:17
  309.7 1.0 reshape.137
  310.7 1.2 gather_fusion
  (96 shorter events, 17.8 us)
Async XLA Ops:
  7.2 166.2 %copy-start = (bf16[1,4096,256]{2,1,0:T(8,128)(2,1)S(1)}, bf16[1,4096,256]{2,1,0:T(8,128)(2,1)}, u32[]{:S(2)}) copy-start(bf16[1,4096,256]{2,1,0:T(8,128)(2,1)} %param.11) | copy-start | bytes 6291460
  7.2 4.4 %copy-start.12 = (bf16[4,2]{0,1:T(2,128)(2,1)S(1)}, bf16[4,2]{0,1:T(2,128)(2,1)}, u32[]{:S(2)}) copy-start(bf16[4,2]{0,1:T(2,128)(2,1)} %param.10) | copy-start | bytes 52
  7.2 128.8 %all-gather.2.cloned.1.call-start = ((), (), s32[]{:S(2)}) async-start(), calls=%async_computation.3 | async-start | bytes 7188480 | tf_op jit(solution)/shard_map/all_gather | solution.py:33
  93.8 154.7 %reduce-scatter.2.cloned.1.call-start = ((), (), s32[]{:S(2)}) async-start(), calls=%async_computation.4 | async-start | bytes 7077888 | tf_op jit(solution)/shard_map/reduce_scatter | solution.py:121
  160.0 7.5 %slice-start = ((bf16[16,8,3,8193]{3,0,2,1:T(8,128)(2,1)}), bf16[16,8,3,1]{3,0,2,1:T(8,128)(2,1)S(1)}, s32[]{:S(2)}) async-start(bf16[16,8,3,8193]{3,0,2,1:T(8,128)(2,1)} %all-gather.2.cloned.1.call-done), calls=%async_computation.5 | async-start | bytes 196608 | tf_op jit(solution)/shard_map/split | solution.py:34
  168.0 4.0 %copy-start.4 = (bf16[384,4096]{1,0:T(8,128)(2,1)S(1)}, bf16[384,4096]{1,0:T(8,128)(2,1)}, u32[]{:S(2)}) copy-start(bf16[384,4096]{1,0:T(8,128)(2,1)} %reshape.132) | copy-start | bytes 9437188
  168.0 4.1 %copy-start.13 = (bf16[1,256,4096]{2,1,0:T(8,128)(2,1)S(1)}, bf16[1,256,4096]{2,1,0:T(8,128)(2,1)}, u32[]{:S(2)}) copy-start(bf16[1,256,4096]{2,1,0:T(8,128)(2,1)} %param.13) | copy-start | bytes 6291460
  172.1 1.3 copy-start.9
  172.1 2.0 copy-start.2
  176.3 1.0 copy-start.7
  176.3 1.7 copy-start.6
  200.5 0.7 copy-start.14
  251.1 57.7 %all-to-all-start.1 = ((f32[16,3,4097]{2,1,0:T(4,128)}), f32[16,3,4097]{2,1,0:T(4,128)S(1)}, u32[]{:S(2)}, u32[]{:S(2)}) async-start(f32[16,3,4097]{2,1,0:T(4,128)} %copy.159), calls=%async_computation.2 | async-start | bytes 2162688 | tf_op jit(solution)/shard_map/all_to_all | solution.py:17
  263.3 4.7 %copy-start.3 = (bf16[384,4096]{1,0:T(8,128)(2,1)S(1)}, bf16[384,4096]{1,0:T(8,128)(2,1)}, u32[]{:S(2)}) copy-start(bf16[384,4096]{1,0:T(8,128)(2,1)} %reshape.133) | copy-start | bytes 9437188
  263.3 4.7 %copy-start.8 = (bf16[384,256]{0,1:T(8,128)(2,1)S(1)}, bf16[384,256]{0,1:T(8,128)(2,1)}, u32[]{:S(2)}) copy-start(bf16[384,256]{0,1:T(8,128)(2,1)} %copy-done.7) | copy-start | bytes 589828
  268.0 2.6 copy-start.5
  268.0 2.6 copy-start.10
  268.0 2.6 copy-start.11
  270.6 45.1 %copy-start.1 = (bf16[1,4096,256]{2,1,0:T(8,128)(2,1)S(1)}, bf16[1,4096,256]{2,1,0:T(8,128)(2,1)}, u32[]{:S(2)}) copy-start(bf16[1,4096,256]{2,1,0:T(8,128)(2,1)} %param.11) | copy-start | bytes 6291460
Sparse Core Ops, SparseCore 0:
  93.9 42.0 all-gather.1
  200.7 47.7 reduce-scatter.1
where the time goes:
time: 328 us; the launch traced here: 323 us
  waiting for transfers between devices  103 us (31%)
  blocking collectives  99.7 us (30%)
  local copies, waits for them, and re-layouts  65.7 us (20%)
  matrix products  24 us (7%)
  between operations  14.4 us (4%)
  starting transfers between devices  12.2 us (4%)
  other arithmetic  3.96 us (1%)
    all_to_all x1, blocking collectives, sent_together(): lax.all_to_all(both, axis, split_axis=split_dim, concat_axis=concat_dim,...  78.7 us
    all_gather x1, waiting for transfers between devices, in_one_piece(): result = lax.all_gather(both, axis, axis=dim, tiled=True)  42.1 us
    all_to_all x1, waiting for transfers between devices, sent_together(): lax.all_to_all(both, axis, split_axis=split_dim, concat_axis=concat_dim,...  35.6 us
    reduce_scatter x1, waiting for transfers between devices, per_device(): lax.psum_scatter(part_dx.reshape(owners, holders, CAP, width), ('tensor',...  24.7 us
    unnamed x1, blocking collectives  21 us
    reshape x2, local copies, waits for them, and re-layouts, per_device(): part_dx.reshape(owners, holders, CAP, width)  18.8 us
    split x5, local copies, waits for them, and re-layouts, in_one_piece(): jnp.split(result, [sum(widths[:k]) for k in range(1, len(widths))], axis=...  16.6 us
    dot_general x6, matrix products, contract(): lax.dot_general(left, right, (((left_dim,), (right_dim,)), ((), ())), pre...  15.9 us
  transfers between devices with their start and end apart: 3, of which 3 were waited for; matrix products, arithmetic and copies ran while one was open for 4% of the time, Pallas kernels for 0%

commit v1 on v0

v1 whole, which is shorter than its diff:
```python
import functools
import jax
import jax.numpy as jnp
from jax import lax
from jax.experimental import pallas as pl
from jax.experimental.pallas import tpu as pltpu
from jax.sharding import PartitionSpec as P

EXPERTS = 4
TOP = 2
LANES = 128
MESH = pl.DeviceIdType.MESH


def places():
    z, x, c = lax.axis_index("expert"), lax.axis_index("tensor"), lax.axis_index("seq")
    ring, line = lax.axis_size("expert"), lax.axis_size("tensor")
    along_z = ({"expert": lax.rem(z + 1, ring)}, {"expert": lax.rem(z + ring - 1, ring)})
    along_x = ({"tensor": lax.rem(x + 1, line)}, {"tensor": lax.rem(x + line - 1, line)})
    return z, x, c, along_z, along_x, {"seq": 1 - c}


def greet(devices):
    barrier = pltpu.get_barrier_semaphore()
    for device in devices:
        pl.semaphore_signal(barrier, inc=1, device_id=device, device_id_type=MESH)
    pl.semaphore_wait(barrier, len(devices))


class Wires:
    def __init__(self, send_sem, recv_sem):
        self.send_sem, self.recv_sem, self.at, self.sent = send_sem, recv_sem, {}, []

    def copy(self, name, src, dst, device):
        k = self.at.setdefault(name, len(self.at))
        return pltpu.make_async_remote_copy(
            src_ref=src,
            dst_ref=dst,
            send_sem=self.send_sem.at[k],
            recv_sem=self.recv_sem.at[k],
            device_id=device,
            device_id_type=MESH,
        )

    def send(self, name, src, dst, device):
        copy = self.copy(name, src, dst, device)
        copy.start()
        self.sent.append(copy)

    def arrived(self, name, ref, device):
        self.copy(name, ref, ref, device).wait_recv()

    def drain(self):
        for copy in self.sent:
            copy.wait_send()


def split_score(score):
    high = score.astype(jnp.bfloat16)
    rest = (score - high.astype(jnp.float32)).astype(jnp.bfloat16)
    lanes = lax.broadcasted_iota(jnp.int32, score.shape, score.ndim - 1)
    return jnp.where(lanes < LANES // 2, high.astype(jnp.float32), rest.astype(jnp.float32))


def joined_score(block):
    return block + pltpu.roll(block, LANES // 2, 1)


def pack(rows):
    score = split_score(joined_score(rows[:, -LANES:]))
    return jnp.concatenate([rows[:, :-LANES], score], axis=1).astype(jnp.bfloat16)


def cut(columns):
    first = columns // 2 // LANES * LANES
    return ((0, first), (first, columns - first))


def gather_kernel(xy_ref, x_out, dy_out, table_out, inc, buf_a, buf_b, send_sem, recv_sem, out_sem):
    z, x, c, along_z, along_x, partner = places()
    ring, line = buf_a.shape[1], buf_a.shape[2]
    half = ring // 2
    wide, narrow = buf_a.shape[-1], buf_b.shape[-1]
    cut_a, cut_b = cut(wide), cut(narrow)
    wires = Wires(send_sem, recv_sem)
    greet((partner, *along_z, *along_x))

    def slabs(k):
        if k == 0:
            return (z,)
        if k == half:
            return (lax.rem(z + half, ring),)
        return (lax.rem(z + ring - k, ring), lax.rem(z + k, ring))

    def block(s, y):
        return buf_a.at[c, s, lax.rem(y + line, line)]

    def part(s, y, d):
        return buf_a.at[c, s, lax.rem(y + line, line), :, pl.ds(*cut_a[d])]

    def to_x(s, key):
        for d in (0, 1):
            wires.send(("x", d, key), block(s, x), block(s, x), along_x[d])

    def x_on(s, key):
        for d, y in ((0, x - 1), (1, x + 1)):
            wires.arrived(("x", d, key), block(s, y), along_x[d])
            wires.send(("h", d, key), part(s, y, d), part(s, y, d), along_x[d])

    def x_end(s, key):
        for d in (0, 1):
            wires.arrived(("h", d, key), part(s, x + 2, d), along_x[d])
        wires.send(("da", key), buf_a.at[c, s], buf_a.at[c, s], partner)

    def b_part(s, d):
        return buf_b.at[c, s, :, :, pl.ds(*cut_b[d])]

    def to_z(s, d, k):
        if k < half:
            wires.send(("za", d, k), block(s, x), block(s, x), along_z[d])
        else:
            wires.send(("za", d, k), part(s, x, d), part(s, x, d), along_z[d])

    def to_z_b(s, d, k):
        ref = buf_b.at[c, s] if k < half else b_part(s, d)
        wires.send(("zb", d, k), ref, ref, along_z[d])

    wires.send("pair", xy_ref.at[1 - c], inc, partner)
    wires.arrived("pair", inc, partner)
    merged = xy_ref[c] + inc[...]
    buf_a[c, z, x] = merged[:, :wide]
    buf_b[c, z, x] = merged[:, wide:]

    def narrow_block(y):
        return buf_b.at[c, z, lax.rem(y + line, line)]

    def narrow_part(y, d):
        return buf_b.at[c, z, lax.rem(y + line, line), :, pl.ds(*cut_b[d])]

    for d in (0, 1):
        wires.send(("b", d), narrow_block(x), narrow_block(x), along_x[d])
    for d in (0, 1):
        to_z(z, d, 1)
    to_x(z, (0, 0))
    for d, y in ((0, x - 1), (1, x + 1)):
        wires.arrived(("b", d), narrow_block(y), along_x[d])
        wires.send(("bh", d), narrow_part(y, d), narrow_part(y, d), along_x[d])
    for d in (0, 1):
        wires.arrived(("bh", d), narrow_part(x + 2, d), along_x[d])
    for d in (0, 1):
        to_z_b(z, d, 1)
    wires.send(("db", (0, 0)), buf_b.at[c, z], buf_b.at[c, z], partner)

    for k in range(1, half + 3):
        if k < half:
            for d, s in enumerate(slabs(k)):
                wires.arrived(("za", d, k), block(s, x), along_z[d])
                to_z(s, d, k + 1)
                to_x(s, (k, d))
            for d, s in enumerate(slabs(k)):
                wires.arrived(("zb", d, k), buf_b.at[c, s], along_z[d])
                to_z_b(s, d, k + 1)
                wires.send(("db", (k, d)), buf_b.at[c, s], buf_b.at[c, s], partner)
        elif k == half:
            (s,) = slabs(k)
            for d in (0, 1):
                wires.arrived(("za", d, k), part(s, x, d), along_z[d])
            to_x(s, (k, 0))
            for d in (0, 1):
                wires.arrived(("zb", d, k), b_part(s, d), along_z[d])
            wires.send(("db", (k, 0)), buf_b.at[c, s], buf_b.at[c, s], partner)
        if 0 <= k - 1 <= half:
            for d, s in enumerate(slabs(k - 1)):
                x_on(s, (k - 1, d))
        if 0 <= k - 2 <= half:
            for d, s in enumerate(slabs(k - 2)):
                x_end(s, (k - 2, d))

    for k in range(half + 1):
        for d, s in enumerate(slabs(k)):
            wires.arrived(("da", (k, d)), buf_a.at[1 - c, s], partner)
            wires.arrived(("db", (k, d)), buf_b.at[1 - c, s], partner)
    width = x_out.shape[-1]
    head = wide - LANES
    outs = []
    for m, out in ((0, x_out), (1, dy_out)):
        outs.append((buf_a.at[m, :, :, :, pl.ds(0, head)], out.at[:, :, :, pl.ds(0, head)]))
        outs.append((buf_b.at[m], out.at[:, :, :, pl.ds(head, narrow)]))
    outs.append((buf_a.at[1, :, :, :, pl.ds(head, LANES)], table_out))
    copies = [pltpu.make_async_copy(a, b, out_sem.at[i]) for i, (a, b) in enumerate(outs)]
    for copy in copies:
        copy.start()
    wires.drain()
    for copy in copies:
        copy.wait()


def gather_rows(xy, wide):
    ring, line = lax.axis_size("expert"), lax.axis_size("tensor")
    rows, columns = xy.shape[1:]
    width = columns - LANES
    narrow = columns - wide
    half = ring // 2
    wires = 1 + 4 + 4 * half + 4 * ring + 2 * ring
    whole = jax.ShapeDtypeStruct((ring, line, rows, width), xy.dtype)
    return pl.pallas_call(
        gather_kernel,
        out_shape=(whole, whole, jax.ShapeDtypeStruct((ring, line, rows, LANES), xy.dtype)),
        in_specs=[pl.BlockSpec(memory_space=pltpu.VMEM)],
        out_specs=(pl.BlockSpec(memory_space=pl.ANY),) * 3,
        scratch_shapes=[
            pltpu.VMEM((rows, columns), xy.dtype),
            pltpu.VMEM((2, ring, line, rows, wide), xy.dtype),
            pltpu.VMEM((2, ring, line, rows, narrow), xy.dtype),
            pltpu.SemaphoreType.DMA((wires,)),
            pltpu.SemaphoreType.DMA((wires,)),
            pltpu.SemaphoreType.DMA((5,)),
        ],
        compiler_params=pltpu.CompilerParams(collective_id=0, has_side_effects=True),
        name="gather_rows",
    )(xy)


def reduce_kernel(part_ref, out_ref, other, mid, mid_in, full, full_in, zs, zs_in, send_sem, recv_sem):
    z, x, c, along_z, along_x, partner = places()
    ring, line = part_ref.shape[1], part_ref.shape[2]
    half = ring // 2
    width = part_ref.shape[-1]
    cuts = cut(width)
    wires = Wires(send_sem, recv_sem)
    greet((partner, *along_z, *along_x))

    def slabs(k):
        if k == 0:
            return (z,)
        if k == half:
            return (lax.rem(z + half, ring),)
        return (lax.rem(z + k, ring), lax.rem(z + ring - k, ring))

    keys = [(k, d) for k in range(half, -1, -1) for d in range(1 if k in (0, half) else 2)]
    slot = {key: i for i, key in enumerate(keys)}

    def chip_sum(s, y):
        y = lax.rem(y + line, line)
        return part_ref[c, s, y].astype(jnp.float32) + other[s, y].astype(jnp.float32)

    def with_part(rows, ref, i, d):
        lo, n = cuts[d]
        added = rows[:, lo : lo + n] + ref[i, :, pl.ds(lo, n)].astype(jnp.float32)
        pieces = [added, rows[:, n:]] if d == 0 else [rows[:, :lo], added]
        return jnp.concatenate(pieces, axis=1)

    def start_x(s, key):
        wires.arrived(("d", key), other.at[s], partner)
        i = slot[key]
        mid[i] = pack(chip_sum(s, x + 2))
        for d, device in ((0, along_x[1]), (1, along_x[0])):
            at = pl.ds(*cuts[d])
            wires.send(("h", d, key), mid.at[i, :, at], mid_in.at[i, :, at], device)

    def middle_x(s, key):
        i = slot[key]
        for d, y, device in ((0, x - 1, along_x[1]), (1, x + 1, along_x[0])):
            wires.arrived(("h", d, key), mid_in.at[i, :, pl.ds(*cuts[d])], device)
            full[d, i] = pack(with_part(chip_sum(s, y), mid_in, i, d))
            wires.send(("f", d, key), full.at[d, i], full_in.at[d, i], device)

    def end_x(s, key):
        i = slot[key]
        for d, device in ((0, along_x[1]), (1, along_x[0])):
            wires.arrived(("f", d, key), full_in.at[d, i], device)
        total = chip_sum(s, x)
        return total + full_in[0, i].astype(jnp.float32) + full_in[1, i].astype(jnp.float32)

    def hop_z(total, k, d):
        if k == half:
            zs[0, k - 1] = pack(total)
            for e in (0, 1):
                at = pl.ds(*cuts[e])
                wires.send(("z", e, k), zs.at[0, k - 1, :, at], zs_in.at[e, k - 1, :, at], along_z[e])
        elif k == half - 1:
            wires.arrived(("z", d, half), zs_in.at[d, half - 1, :, pl.ds(*cuts[d])], along_z[d])
            zs[d, k - 1] = pack(with_part(total, zs_in.at[d], half - 1, d))
            wires.send(("z", d, k), zs.at[d, k - 1], zs_in.at[d, k - 1], along_z[d])
        elif k > 0:
            wires.arrived(("z", d, k + 1), zs_in.at[d, k], along_z[d])
            zs[d, k - 1] = pack(total + zs_in[d, k].astype(jnp.float32))
            wires.send(("z", d, k), zs.at[d, k - 1], zs_in.at[d, k - 1], along_z[d])
        else:
            for e in (0, 1):
                wires.arrived(("z", e, 1), zs_in.at[e, 0], along_z[e])
                total = total + zs_in[e, 0].astype(jnp.float32)
            score = joined_score(total[:, -LANES:])
            out_ref[c] = jnp.concatenate([total[:, :-LANES], score], axis=1)
            wires.send("pair", out_ref.at[c], out_ref.at[c], partner)
            wires.arrived("pair", out_ref.at[1 - c], partner)

    for key in keys:
        s = slabs(key[0])[key[1]]
        wires.send(("d", key), part_ref.at[1 - c, s], other.at[s], partner)
    for k in range(half, -3, -1):
        for j, act in ((k, start_x), (k + 1, middle_x)):
            if 0 <= j <= half:
                for d, s in enumerate(slabs(j)):
                    act(s, (j, d))
        j = k + 2
        if 0 <= j <= half:
            for d, s in enumerate(slabs(j)):
                hop_z(end_x(s, (j, d)), j, d)
    wires.drain()


def reduce_rows(part):
    ring, line, rows, width = part.shape[1:]
    half = ring // 2
    wires = ring + 4 * ring + 2 * half + 1
    return pl.pallas_call(
        reduce_kernel,
        out_shape=jax.ShapeDtypeStruct((2, rows, width), jnp.float32),
        in_specs=[pl.BlockSpec(memory_space=pltpu.VMEM)],
        out_specs=pl.BlockSpec(memory_space=pltpu.VMEM),
        scratch_shapes=[
            pltpu.VMEM((ring, line, rows, width), part.dtype),
            pltpu.VMEM((ring, rows, width), part.dtype),
            pltpu.VMEM((ring, rows, width), part.dtype),
            pltpu.VMEM((2, ring, rows, width), part.dtype),
            pltpu.VMEM((2, ring, rows, width), part.dtype),
            pltpu.VMEM((2, half, rows, width), part.dtype),
            pltpu.VMEM((2, half, rows, width), part.dtype),
            pltpu.SemaphoreType.DMA((wires,)),
            pltpu.SemaphoreType.DMA((wires,)),
        ],
        compiler_params=pltpu.CompilerParams(collective_id=1, has_side_effects=True),
        name="reduce_rows",
    )(part)


def silu_parts(gate):
    sigma = jax.nn.sigmoid(gate)
    return (gate * sigma, sigma * (1.0 + gate * (1.0 - sigma)))


def contract(left, right, left_dim, right_dim):
    return lax.dot_general(
        left, right, (((left_dim,), (right_dim,)), ((), ())), preferred_element_type=jnp.float32
    )


def per_device(tokens, out_grad, expert_ids, probs, w_gate, w_up, w_down):
    ring, line = lax.axis_size("expert"), lax.axis_size("tensor")
    mine = lax.axis_index("expert") // (ring // EXPERTS)
    core = lax.axis_index("seq")
    count, width = tokens.shape
    lanes = jnp.arange(LANES, dtype=jnp.int32)
    named = expert_ids[:, :, None] == lanes[None, None, :]
    table = jnp.sum(
        jnp.where(named, probs[:, :, None].astype(jnp.float32), 0.0), axis=1
    ).astype(jnp.bfloat16)

    def placed(rows):
        part_a = width * 5 // 8 // LANES * LANES
        rows = jnp.concatenate([rows[:, :part_a], table, rows[:, part_a:]], axis=1)
        zero = jnp.zeros_like(rows)
        first, second = jnp.concatenate([rows, zero]), jnp.concatenate([zero, rows])
        return jnp.where(core == 0, first, second)

    wide = width * 5 // 8 // LANES * LANES + LANES
    x_all, dy_all, tables = gather_rows(jnp.stack([placed(tokens), placed(out_grad)]), wide)
    inputs, cotangent = x_all.reshape(-1, width), dy_all.reshape(-1, width)
    tables = tables.reshape(-1, LANES).astype(jnp.float32)
    scale = jnp.sum(jnp.where(lanes[None] == mine, tables, 0.0), axis=1)[:, None]
    w_g, w_u, w_d = w_gate[0], w_up[0], w_down[0]
    gate = jnp.dot(inputs, w_g, preferred_element_type=jnp.float32)
    up = jnp.dot(inputs, w_u, preferred_element_type=jnp.float32)
    back = contract(cotangent, w_d, 1, 1)
    act, slope = silu_parts(gate)
    hidden = act * up
    score = jnp.sum(back * hidden, axis=1)
    scaled = scale * back
    d_gate = (scaled * up * slope).astype(jnp.bfloat16)
    d_up = (scaled * act).astype(jnp.bfloat16)
    weighted = (scale * hidden).astype(jnp.bfloat16)
    part_dx = (contract(d_gate, w_g, 1, 1) + contract(d_up, w_u, 1, 1)).astype(jnp.bfloat16)
    part_score = jnp.where(lanes[None] % (LANES // 2) == mine, score[:, None], 0.0)
    high = lax.reduce_precision(part_score, 8, 7)
    part_score = jnp.where(lanes[None] < LANES // 2, high, part_score - high).astype(jnp.bfloat16)
    side = width // 2
    part = jnp.stack(
        [
            jnp.concatenate([part_dx[:, :side], part_score], axis=1),
            jnp.concatenate([part_dx[:, side:], part_score], axis=1),
        ]
    )
    total = reduce_rows(part.reshape(2, ring, line, -1, side + LANES))
    total = jnp.where(core == 0, total[:, :count], total[:, count:])
    grad_tokens = jnp.concatenate([total[0, :, :side], total[1, :, :side]], axis=1)
    grad_probs = jnp.sum(jnp.where(named, total[0, :, None, side:], 0.0), axis=2)
    grad_g = contract(inputs, d_gate, 0, 0).astype(jnp.bfloat16)[None]
    grad_u = contract(inputs, d_up, 0, 0).astype(jnp.bfloat16)[None]
    grad_d = contract(weighted, cotangent, 0, 0).astype(jnp.bfloat16)[None]
    return (grad_tokens, grad_probs, grad_g, grad_u, grad_d)


def solution(mesh):
    rows = P(("parts", "expert", "tensor", "seq"), None)
    return jax.shard_map(
        per_device,
        mesh=mesh,
        in_specs=(
            rows,
            rows,
            rows,
            rows,
            P("expert", None, ("tensor", "seq")),
            P("expert", None, ("tensor", "seq")),
            P("expert", ("tensor", "seq"), None),
        ),
        out_specs=(
            rows,
            rows,
            P(("parts", "expert"), None, ("tensor", "seq")),
            P(("parts", "expert"), None, ("tensor", "seq")),
            P(("parts", "expert"), ("tensor", "seq"), None),
        ),
        check_vma=False,
    )
```

time: 328 us -> 152 us (0.46); the launches traced: 323 us -> 151 us
  Pallas kernels: 0 us -> 119 us
  waiting for transfers between devices: 103 us -> 0 us
  blocking collectives: 99.7 us -> 0 us
  local copies, waits for them, and re-layouts: 65.7 us -> 4.66 us
  between operations: 14.4 us -> 0.83 us
  starting transfers between devices: 12.2 us -> 0 us
  matrix products: 24 us -> 18 us
  other arithmetic: 3.96 us -> 8.78 us
    pallas_call x0 -> x2, Pallas kernels: none -> 119 us  [the longest x1 77.3 us: gather_rows(): pl.pallas_call(gather_kernel, out_shape=(whole, whole, jax.ShapeDtypeStru...]
    all_to_all x1 -> x0, blocking collectives: 78.7 us -> none  [sent_together(): lax.all_to_all(both, axis, split_axis=split_dim, concat_axis=concat_dim,...]
    all_gather x1 -> x0, waiting for transfers between devices: 42.1 us -> none  [in_one_piece(): result = lax.all_gather(both, axis, axis=dim, tiled=True)]
    all_to_all x1 -> x0, waiting for transfers between devices: 35.6 us -> none  [sent_together(): lax.all_to_all(both, axis, split_axis=split_dim, concat_axis=concat_dim,...]
    reshape x11 -> x0, local copies, waits for them, and re-layouts: 35.4 us -> none  [the longest x2 18.8 us: per_device(): part_dx.reshape(owners, holders, CAP, width)]
    reduce_scatter x1 -> x0, waiting for transfers between devices: 24.7 us -> none  [per_device(): lax.psum_scatter(part_dx.reshape(owners, holders, CAP, width), ('tensor',...]
    unnamed x1 -> x0, blocking collectives: 21 us -> none
    split x5 -> x0, local copies, waits for them, and re-layouts: 16.6 us -> none  [in_one_piece(): jnp.split(result, [sum(widths[:k]) for k in range(1, len(widths))], axis=...]
  transfers between devices with their start and end apart: 3 -> 0, of which waited for: 3 -> 0; matrix products, arithmetic and copies ran while one was open for 4% -> 0% of each run, Pallas kernels for 0% -> 0%
where the time goes in v1:
time: 152 us; the launch traced here: 151 us
  Pallas kernels  119 us (78%)
  matrix products  18 us (12%)
  other arithmetic  8.78 us (6%)
  local copies, waits for them, and re-layouts  4.66 us (3%)
    pallas_call x1, Pallas kernels, gather_rows(): pl.pallas_call(gather_kernel, out_shape=(whole, whole, jax.ShapeDtypeStru...  77.3 us
    pallas_call x1, Pallas kernels, reduce_rows(): pl.pallas_call(reduce_kernel, out_shape=jax.ShapeDtypeStruct((2, rows, wi...  41.6 us
    dot_general x6, matrix products, contract(): lax.dot_general(left, right, (((left_dim,), (right_dim,)), ((), ())), pre...  12.1 us
    dot_general x1, matrix products, per_device(): up = jnp.dot(inputs, w_u, preferred_element_type=jnp.float32)  4.29 us

profile of v1, /device:TPU:33, one launch (start us, length us, event | category | flops | bytes accessed | tf_op | source)
XLA Modules:
  0.0 151.2 jit_solution(5148922251158054889)
XLA Ops:
  0.7 0.8 convert_element_type.35
  1.5 0.8 select_reduce_fusion.2
  2.3 0.7 slice.34
  3.0 0.7 slice.36
  3.7 0.7 slice.33
  4.4 0.7 slice.35
  5.3 0.7 pad_maximum_fusion.3.xy_ref
  5.9 77.3 %gather_rows.1 = (bf16[16,4,8,4096]{3,2,1,0:T(8,128)(2,1)}, bf16[16,4,8,4096]{3,2,1,0:T(8,128)(2,1)}, bf16[16,4,8,128]{3,2,1,0:T(8,128)(2,1)}) custom-call(bf16[2,8,4224]{2,1,0:T(8,128)(2,1)} %pad_maximum_fusion.3.xy_ref), custom_call_target="tpu_custom_call" | custom-call | tf_op jit(solution)/shard_map/gather_rows/pallas_call | solution.py:206
  83.3 1.1 select_reduce_fusion
  84.5 4.3 %fusion.8 = f32[512,256]{0,1:T(8,128)S(1)} fusion(bf16[512,4096]{1,0:T(8,128)(2,1)} %bitcast.45, bf16[1,4096,256]{2,1,0:T(8,128)(2,1)} %param.12), kind=kOutput, calls=%fused_computation.15 | convolution fusion | flops 1073741824 | bytes 6815744 | tf_op jit(solution)/shard_map/dot_general | solution.py:374
  89.2 1.3 fusion.10
  90.5 0.8 copy-done.1
  91.4 1.6 %multiply_convert_fusion.2 = (bf16[512,256]{0,1:T(8,128)(2,1)S(1)}, f32[512]{0:T(512)S(1)}, bf16[512,256]{0,1:T(8,128)(2,1)S(1)}, f32[512,256]{0,1:T(8,128)S(1)}) fusion(f32[512,256]{0,1:T(8,128)S(1)} %fusion.8, f32[512,256]{0,1:T(8,128)S(1)} %fusion.10, f32[512]{0:T(512)S(1)} %mul.40, bf16[512,4096]{1,0:T(8,128)(2,1)S(1)} %bitcast.46, ...), kind=kOutput, calls=%fused_computation.22 | convolution fusion | flops 1075969536 | bytes 8392704 | tf_op jit(solution)/shard_map/dot_general | solution.py:373
  93.0 2.6 %fusion.2 = bf16[1,256,4096]{2,1,0:T(8,128)(2,1)} fusion(bf16[512,4096]{1,0:T(8,128)(2,1)S(1)} %bitcast.52, f32[512]{0:T(512)S(1)} %mul.40, f32[512,256]{0,1:T(8,128)S(1)} %fusion.8, f32[512,256]{0,1:T(8,128)S(1)} %get-tuple-element.22), kind=kOutput, calls=%fused_computation.6 | convolution fusion | flops 1075707904 | bytes 7342080 | tf_op jit(solution)/shard_map/dot_general | solution.py:344
  95.8 2.6 %fusion = bf16[1,4096,256]{2,1,0:T(8,128)(2,1)} fusion(bf16[512,4096]{1,0:T(8,128)(2,1)S(1)} %bitcast.47, bf16[512,256]{0,1:T(8,128)(2,1)S(1)} %get-tuple-element.13), kind=kOutput, calls=%fused_computation.4 | convolution fusion | flops 1074790400 | bytes 6553600 | tf_op jit(solution)/shard_map/dot_general | solution.py:344
  98.4 2.6 %fusion.1 = bf16[1,4096,256]{2,1,0:T(8,128)(2,1)} fusion(bf16[512,4096]{1,0:T(8,128)(2,1)S(1)} %bitcast.48, bf16[512,256]{0,1:T(8,128)(2,1)S(1)} %get-tuple-element.15), kind=kOutput, calls=%fused_computation.5 | convolution fusion | flops 1074790400 | bytes 6553600 | tf_op jit(solution)/shard_map/dot_general | solution.py:344
  101.0 1.5 %fusion.3 = f32[512,4096]{1,0:T(8,128)S(1)} fusion(bf16[512,256]{0,1:T(8,128)(2,1)S(1)} %get-tuple-element.13, bf16[1,4096,256]{2,1,0:T(8,128)(2,1)S(1)} %copy-done), kind=kOutput, calls=%fused_computation.10 | convolution fusion | flops 1073741824 | bytes 10747904 | tf_op jit(solution)/shard_map/dot_general | solution.py:344
  102.6 1.3 add_convert_fusion
  104.3 0.4 pad_maximum_fusion.2
  104.7 2.5 %pad_maximum_fusion.part_ref = bf16[2,16,4,8,2176]{4,3,2,1,0:T(8,128)(2,1)} fusion(bf16[1,16,4,8,2176]{4,3,2,1,0:T(8,128)(2,1)S(1)} %bitcast.50, bf16[1,16,4,8,2176]{4,3,2,1,0:T(8,128)(2,1)S(1)} %bitcast.49), kind=kLoop, calls=%fused_computation.7 | loop fusion | flops 2228224 | bytes 8912896 | tf_op jit(solution)/shard_map/stack | solution.py:388
  107.2 41.6 %reduce_rows.1 = f32[2,8,2176]{2,1,0:T(8,128)} custom-call(bf16[2,16,4,8,2176]{4,3,2,1,0:T(8,128)(2,1)} %pad_maximum_fusion.part_ref), custom_call_target="tpu_custom_call" | custom-call | tf_op jit(solution)/shard_map/reduce_rows/pallas_call | solution.py:317
  148.8 1.0 slice_select_fusion
  149.9 0.7 select_reduce_fusion.1
  150.6 0.6 pad_maximum_fusion.4
  (20 shorter events, 1.2 us)
Async XLA Ops:
  0.6 89.9 %copy-start = (bf16[1,4096,256]{2,1,0:T(8,128)(2,1)S(1)}, bf16[1,4096,256]{2,1,0:T(8,128)(2,1)}, u32[]{:S(2)}) copy-start(bf16[1,4096,256]{2,1,0:T(8,128)(2,1)} %param.11) | copy-start | bytes 6291460
  84.4 4.3 %copy-start.4 = (bf16[16,4,8,4096]{3,2,1,0:T(8,128)(2,1)S(1)}, bf16[16,4,8,4096]{3,2,1,0:T(8,128)(2,1)}, u32[]{:S(2)}) copy-start(bf16[16,4,8,4096]{3,2,1,0:T(8,128)(2,1)} %get-tuple-element.9) | copy-start | bytes 12582916
  84.5 4.7 %copy-start.5 = (bf16[1,256,4096]{2,1,0:T(8,128)(2,1)S(1)}, bf16[1,256,4096]{2,1,0:T(8,128)(2,1)}, u32[]{:S(2)}) copy-start(bf16[1,256,4096]{2,1,0:T(8,128)(2,1)} %param.13) | copy-start | bytes 6291460
  89.2 2.2 %copy-start.1 = (bf16[16,4,8,4096]{3,2,1,0:T(8,128)(2,1)S(1)}, bf16[16,4,8,4096]{3,2,1,0:T(8,128)(2,1)}, u32[]{:S(2)}) copy-start(bf16[16,4,8,4096]{3,2,1,0:T(8,128)(2,1)} %get-tuple-element.10) | copy-start | bytes 12582916
  101.0 1.6 %copy-start.2 = (bf16[1,4096,256]{2,1,0:T(8,128)(2,1)S(1)}, bf16[1,4096,256]{2,1,0:T(8,128)(2,1)}, u32[]{:S(2)}) copy-start(bf16[1,4096,256]{2,1,0:T(8,128)(2,1)} %param.12) | copy-start | bytes 6291460
  107.2 42.7 %copy-start.3 = (s32[4,2]{0,1:T(2,128)S(1)}, s32[4,2]{0,1:T(2,128)}, u32[]{:S(2)}) copy-start(s32[4,2]{0,1:T(2,128)} %param.9) | copy-start | bytes 100
